TPU v7x, 16 devices: a whole 2x2x2 slice. The times are simulated.
16 devices in a mesh: rep: 1, r: 2 (over z), s: 8 (over x, y, core).
Axes of the slice: x: 2, y: 2, z: 2, core: 2. Of those that a mesh axis runs over, the one named last changes fastest.
Arguments:
- x: bfloat16 [16, 2048, 768], P(('rep', 'r', 's'))
- dy: bfloat16 [16, 2048, 768], P(('rep', 'r', 's'))
- w_gate: bfloat16 [2, 768, 6144], P(None, 's')
- w_up: bfloat16 [2, 768, 6144], P(None, 's')
- w_down: bfloat16 [2, 6144, 768], P(None, 's')
Outputs:
- output 1: bfloat16 [16, 2048, 768], P(('rep', 'r', 's'))
- output 2: bfloat16 [2, 768, 6144], P('rep', 's')
- output 3: bfloat16 [2, 768, 6144], P('rep', 's')
- output 4: bfloat16 [2, 6144, 768], P('rep', 's')
All inputs are finite; a program needn't handle non-finite values.
Results may differ from a plain program's by a relative error of at most 0.018.
Values are sent between devices in bfloat16 or wider.
A program may use at most 2 GiB of HBM per device.

v0:
```python
import jax
import jax.numpy as jnp
from jax import lax
from jax.sharding import PartitionSpec as P

NAMES = ("w_gate", "w_up", "w_down")


def matmul(a, w):
    return jnp.dot(a, w, preferred_element_type=jnp.float32).astype(jnp.bfloat16)


def normed(h):
    wide = h.astype(jnp.float32)
    scale = lax.rsqrt(jnp.mean(wide**2, -1, keepdims=True) + 1e-6)
    return (wide * scale).astype(jnp.bfloat16)


def layer(h, w):
    a = normed(h)
    gate = jnp.dot(a, w["w_gate"], preferred_element_type=jnp.float32)
    up = jnp.dot(a, w["w_up"], preferred_element_type=jnp.float32)
    return h + matmul((jax.nn.silu(gate) * up).astype(jnp.bfloat16), w["w_down"])


def solution(mesh):
    def fetched(weights, number):
        return {name: lax.all_gather(w[number], "s", axis=0, tiled=True) for name, w in zip(NAMES, weights, strict=True)}

    def summed(term):
        return lax.psum(lax.psum_scatter(term, "s", scatter_dimension=0, tiled=True), "r")

    def step(x, dy, *weights):
        layers = weights[0].shape[0]
        h, inputs = x[0], []
        for number in range(layers):
            inputs.append(h)
            h = layer(h, fetched(weights, number))
        by_h, mine = dy[0], [None] * layers
        for number in reversed(range(layers)):
            _, back = jax.vjp(lambda w, h: layer(h, w), fetched(weights, number), inputs[number])
            by_w, by_h = back(by_h)
            mine[number] = [summed(by_w[name]) for name in NAMES]
        return (by_h[None], *(jnp.stack([mine[number][i] for number in range(layers)]) for i in range(3)))

    states, cut = P(("rep", "r", "s"), None, None), P(None, "s", None)
    return jax.shard_map(
        step,
        mesh=mesh,
        in_specs=(states, states) + (cut,) * 3,
        out_specs=(states,) + (P("rep", "s", None),) * 3,
        check_vma=False,
    )
```

profile of v0, /device:TPU:0, one launch (start us, length us, event | category | flops | bytes accessed | tf_op | source)
XLA Modules:
  0.0 1128.9 jit_solution(15489786244523737546)
XLA Ops:
  26.9 41.4 %all-gather.13.cloned.1.call-done = bf16[1,768,6144]{2,1,0:T(8,128)(2,1)} async-done(((bf16[1,96,6144]{2,1,0:T(8,128)(2,1)}), bf16[1,768,6144]{2,1,0:T(8,128)(2,1)}) %all-gather.13.cloned.1.call-update) | async-done | bytes 9437200 | tf_op jit(solution)/shard_map/all_gather | solution.py:28
  68.4 28.8 %fusion.30 = f32[2048,6144]{1,0:T(8,128)} fusion(bf16[1,768,6144]{2,1,0:T(8,128)(2,1)} %all-gather.13.cloned.1.call-done, bf16[1,2048,768]{1,2,0:T(8,128)(2,1)S(1)} %copy.10, f32[2048]{0:T(1024)S(1)} %fusion.78), kind=kOutput, calls=%fused_computation.53 | convolution fusion | flops 19332071424 | bytes 62922752 | tf_op jit(solution)/shard_map/dot_general | solution.py:21
  97.2 28.4 %all-gather.15.cloned.1.call-done = bf16[1,768,6144]{2,1,0:T(8,128)(2,1)} async-done(((bf16[1,96,6144]{2,1,0:T(8,128)(2,1)}), bf16[1,768,6144]{2,1,0:T(8,128)(2,1)}) %all-gather.15.cloned.1.call-update) | async-done | bytes 9437200 | tf_op jit(solution)/shard_map/all_gather | solution.py:28
  125.6 50.1 %multiply_convert_fusion.1 = (bf16[2048,6144]{1,0:T(8,128)(2,1)}, f32[2048,6144]{1,0:T(8,128)}) fusion(f32[2048,6144]{1,0:T(8,128)} %fusion.30, bf16[1,768,6144]{2,1,0:T(8,128)(2,1)} %all-gather.15.cloned.1.call-done, bf16[1,2048,768]{1,2,0:T(8,128)(2,1)S(1)} %copy.10, f32[2048]{0:T(1024)S(1)} %fusion.78), kind=kOutput, calls=%fused_computation.13 | convolution fusion | flops 19407568896 | bytes 138420224 | tf_op jit(solution)/shard_map/dot_general | solution.py:22
  182.3 27.1 %fusion.39 = (f32[2048]{0:T(1024)S(1)}, bf16[2048,768]{0,1:T(8,128)(2,1)}) fusion(bf16[2048,6144]{1,0:T(8,128)(2,1)} %get-tuple-element.20, bf16[1,6144,768]{2,1,0:T(8,128)(2,1)} %all-gather.17.cloned.1.call-done, bf16[1,2048,768]{1,2,0:T(8,128)(2,1)S(1)} %copy.10), kind=kOutput, calls=%fused_computation.64 | convolution fusion | flops 19335215104 | bytes 40902656 | tf_op jit(solution)/shard_map/dot_general | solution.py:10
  209.4 29.3 %all-gather.21.cloned.1.call-done = bf16[1,6144,768]{2,1,0:T(8,128)(2,1)} async-done(((bf16[1,768,768]{2,1,0:T(8,128)(2,1)}), bf16[1,6144,768]{2,1,0:T(8,128)(2,1)}) %all-gather.21.cloned.1.call-update) | async-done | bytes 9437200 | tf_op jit(solution)/shard_map/all_gather | solution.py:28
  238.7 26.5 %convolution_convert_fusion.1 = bf16[2048,6144]{1,0:T(8,128)(2,1)} fusion(bf16[1,6144,768]{2,1,0:T(8,128)(2,1)} %all-gather.21.cloned.1.call-done, bf16[1,2048,768]{2,1,0:T(8,128)(2,1)} %param.6), kind=kOutput, calls=%fused_computation.22 | convolution fusion | flops 19339935744 | bytes 37748736 | tf_op jit(solution)/shard_map/transpose(jvp())/dot_general | solution.py:10
  265.3 30.5 %all-gather.23.cloned.1.call-done = bf16[1,768,6144]{2,1,0:T(8,128)(2,1)} async-done(((bf16[1,96,6144]{2,1,0:T(8,128)(2,1)}), bf16[1,768,6144]{2,1,0:T(8,128)(2,1)}) %all-gather.23.cloned.1.call-update) | async-done | bytes 9437200 | tf_op jit(solution)/shard_map/all_gather | solution.py:28
  295.8 29.2 %fusion.14 = f32[2048,6144]{1,0:T(8,128)} fusion(bf16[1,768,6144]{2,1,0:T(8,128)(2,1)} %all-gather.23.cloned.1.call-done, bf16[2048,768]{0,1:T(8,128)(2,1)S(1)} %copy-done.6, f32[2048]{0:T(1024)S(1)} %fusion.79), kind=kOutput, calls=%fused_computation.37 | convolution fusion | flops 19332071424 | bytes 62922752 | tf_op jit(solution)/shard_map/jvp()/dot_general | solution.py:22
  325.0 27.8 %all-gather.19.cloned.1.call-done = bf16[1,768,6144]{2,1,0:T(8,128)(2,1)} async-done(((bf16[1,96,6144]{2,1,0:T(8,128)(2,1)}), bf16[1,768,6144]{2,1,0:T(8,128)(2,1)}) %all-gather.19.cloned.1.call-update) | async-done | bytes 9437200 | tf_op jit(solution)/shard_map/all_gather | solution.py:28
  352.9 63.9 %fusion.1 = (bf16[2048,6144]{1,0:T(8,128)(2,1)}, f32[2048,6144]{1,0:T(8,128)}) fusion(f32[2048,6144]{1,0:T(8,128)} %fusion.14, bf16[2048,6144]{1,0:T(8,128)(2,1)} %convolution_convert_fusion.1, bf16[1,768,6144]{2,1,0:T(8,128)(2,1)} %all-gather.19.cloned.1.call-done, bf16[2048,768]{0,1:T(8,128)(2,1)S(1)} %copy-done.6, f32[2048]{0:T(1024)S(1)} %fusion.79), kind=kOutput, calls=%fused_computation.7 | convolution fusion | flops 19483066368 | bytes 163586048 | tf_op jit(solution)/shard_map/jvp()/dot_general | solution.py:21
  416.8 33.0 %fusion.45 = bf16[2048,768]{0,1:T(8,128)(2,1)} fusion(bf16[1,768,6144]{2,1,0:T(8,128)(2,1)} %all-gather.23.cloned.1.call-done, bf16[2048,6144]{1,0:T(8,128)(2,1)} %convolution_convert_fusion.1, f32[2048,6144]{1,0:T(8,128)} %get-tuple-element.25), kind=kOutput, calls=%fused_computation.68 | convolution fusion | flops 19404423168 | bytes 88080384 | tf_op jit(solution)/shard_map/transpose(jvp())/dot_general | solution.py:22
  449.8 26.8 %fusion.41 = (f32[2048]{0:T(1024)S(1)}, bf16[2048,768]{0,1:T(8,128)(2,1)S(1)}) fusion(bf16[2048,768]{0,1:T(8,128)(2,1)S(1)} %copy-done.6, bf16[2048,768]{0,1:T(8,128)(2,1)} %fusion.45, bf16[2048,6144]{1,0:T(8,128)(2,1)} %get-tuple-element.24, bf16[1,768,6144]{2,1,0:T(8,128)(2,1)} %all-gather.19.cloned.1.call-done), kind=kOutput, calls=%fused_computation.66 | convolution fusion | flops 19335215104 | bytes 44048384 | tf_op jit(solution)/shard_map/transpose(jvp())/dot_general | solution.py:21
  480.6 26.5 %convolution_convert_fusion.4 = bf16[6144,768]{1,0:T(8,128)(2,1)} fusion(bf16[2048,6144]{1,0:T(8,128)(2,1)} %get-tuple-element.20, bf16[2048,768]{0,1:T(8,128)(2,1)S(1)} %fusion.59), kind=kOutput, calls=%fused_computation.36 | convolution fusion | flops 19332071424 | bytes 37748736 | tf_op jit(solution)/shard_map/transpose(jvp())/dot_general | solution.py:10
  509.0 42.0 %fusion.11 = bf16[6144,768]{1,0:T(8,128)(2,1)} fusion(f32[2048,6144]{1,0:T(8,128)} %fusion.14, bf16[1,2048,768]{2,1,0:T(8,128)(2,1)S(1)} %copy-done.5, f32[2048,6144]{1,0:T(8,128)} %get-tuple-element.25), kind=kOutput, calls=%fused_computation.31 | convolution fusion | flops 19407568896 | bytes 113246208 | tf_op jit(solution)/shard_map/transpose(jvp())/dot_general | solution.py:10
  551.1 63.8 %fusion.3 = (bf16[2048,6144]{1,0:T(8,128)(2,1)}, bf16[2048,6144]{1,0:T(8,128)(2,1)}) fusion(f32[2048,6144]{1,0:T(8,128)} %fusion.30, f32[2048,6144]{1,0:T(8,128)} %get-tuple-element.21, bf16[2048,768]{0,1:T(8,128)(2,1)} %copy-done.3, bf16[1,6144,768]{2,1,0:T(8,128)(2,1)} %all-gather.17.cloned.1.call-done), kind=kOutput, calls=%fused_computation.9 | convolution fusion | flops 19490930688 | bytes 163577856 | tf_op jit(solution)/shard_map/transpose(jvp())/dot_general | solution.py:10
  614.8 32.1 %fusion.12 = bf16[768,6144]{1,0:T(8,128)(2,1)} fusion(bf16[2048,6144]{1,0:T(8,128)(2,1)} %get-tuple-element.29, bf16[1,2048,768]{1,2,0:T(8,128)(2,1)S(1)} %copy-done.1, f32[2048]{0:T(1024)S(1)} %copy-done.11, f32[2048,6144]{1,0:T(8,128)} %fusion.30), kind=kOutput, calls=%fused_computation.34 | convolution fusion | flops 19412287488 | bytes 88088576 | tf_op jit(solution)/shard_map/transpose(jvp())/dot_general | solution.py:22
  647.7 33.1 %fusion.13 = bf16[768,6144]{1,0:T(8,128)(2,1)} fusion(bf16[2048,6144]{1,0:T(8,128)(2,1)} %convolution_convert_fusion.1, bf16[2048,768]{0,1:T(8,128)(2,1)} %get-tuple-element.23, f32[2048]{0:T(1024)S(1)} %copy-done.13, f32[2048,6144]{1,0:T(8,128)} %get-tuple-element.25), kind=kOutput, calls=%fused_computation.35 | convolution fusion | flops 19412287488 | bytes 88088576 | tf_op jit(solution)/shard_map/transpose(jvp())/dot_general | solution.py:22
  732.7 65.4 %reduce-scatter.13.cloned.1.call-done = bf16[96,6144]{1,0:T(8,128)(2,1)} async-done(((bf16[768,6144]{1,0:T(8,128)(2,1)}), bf16[96,6144]{1,0:T(8,128)(2,1)}) %reduce-scatter.13.cloned.1.call-update) | async-done | bytes 1179664 | tf_op jit(solution)/shard_map/reduce_scatter | solution.py:31
  798.2 73.6 %reduce-scatter.9.cloned.1.call-done = bf16[96,6144]{1,0:T(8,128)(2,1)} async-done(((bf16[768,6144]{1,0:T(8,128)(2,1)}), bf16[96,6144]{1,0:T(8,128)(2,1)}) %reduce-scatter.9.cloned.1.call-update) | async-done | bytes 1179664 | tf_op jit(solution)/shard_map/reduce_scatter | solution.py:31
  871.8 73.5 %reduce-scatter.7.cloned.1.call-done = bf16[96,6144]{1,0:T(8,128)(2,1)} async-done(((bf16[768,6144]{1,0:T(8,128)(2,1)}), bf16[96,6144]{1,0:T(8,128)(2,1)}) %reduce-scatter.7.cloned.1.call-update) | async-done | bytes 1179664 | tf_op jit(solution)/shard_map/reduce_scatter | solution.py:31
  945.3 33.0 %fusion.42 = bf16[2048,768]{0,1:T(8,128)(2,1)} fusion(bf16[1,768,6144]{2,1,0:T(8,128)(2,1)} %all-gather.15.cloned.1.call-done, bf16[2048,6144]{1,0:T(8,128)(2,1)} %get-tuple-element.29, f32[2048,6144]{1,0:T(8,128)} %fusion.30), kind=kOutput, calls=%fused_computation.67 | convolution fusion | flops 19404423168 | bytes 88080384 | tf_op jit(solution)/shard_map/transpose(jvp())/dot_general | solution.py:22
  978.3 26.9 %fusion.38 = (f32[2048]{0:T(1024)S(1)}, bf16[2048,768]{0,1:T(8,128)(2,1)S(1)}) fusion(bf16[1,2048,768]{1,2,0:T(8,128)(2,1)S(1)} %copy-done.1, bf16[2048,768]{0,1:T(8,128)(2,1)} %fusion.42, bf16[2048,6144]{1,0:T(8,128)(2,1)} %get-tuple-element.28, bf16[1,768,6144]{2,1,0:T(8,128)(2,1)} %all-gather.13.cloned.1.call-done), kind=kOutput, calls=%fused_computation.63 | convolution fusion | flops 19335215104 | bytes 44048384 | tf_op jit(solution)/shard_map/transpose(jvp())/dot_general | solution.py:21
  1013.7 101.0 %all-reduce.3.cloned.1.call-done = (bf16[1,96,6144]{2,1,0:T(8,128)(2,1)}, bf16[1,96,6144]{2,1,0:T(8,128)(2,1)}, bf16[1,96,6144]{2,1,0:T(8,128)(2,1)}, bf16[1,96,...) async-done(((bf16[1,96,6144]{2,1,0:T(8,128)(2,1)}, bf16[1,96,6144]{2,1,0:T(8,128)(2,1)}, bf16[1,96,6144]{2,1,0:T(8,128)(2,1)}, ...) | async-done | bytes 7077904 | tf_op jit(solution)/shard_map/psum | solution.py:31
  (79 shorter events, 100.4 us)
Async XLA Ops:
  7.2 61.2 %all-gather.13.cloned.1.call-start = ((), (), s32[]{:S(2)}) async-start(), calls=%async_computation.12 | async-start | bytes 10616832 | tf_op jit(solution)/shard_map/all_gather | solution.py:28
  10.7 115.0 %all-gather.15.cloned.1.call-start = ((), (), s32[]{:S(2)}) async-start(), calls=%async_computation.13 | async-start | bytes 10616832 | tf_op jit(solution)/shard_map/all_gather | solution.py:28
  14.0 168.3 %all-gather.17.cloned.1.call-start = ((), (), s32[]{:S(2)}) async-start(), calls=%async_computation.14 | async-start | bytes 10616832 | tf_op jit(solution)/shard_map/all_gather | solution.py:28
  15.6 223.1 %all-gather.21.cloned.1.call-start = ((), (), s32[]{:S(2)}) async-start(), calls=%async_computation.16 | async-start | bytes 10616832 | tf_op jit(solution)/shard_map/all_gather | solution.py:28
  16.2 279.6 %all-gather.23.cloned.1.call-start = ((), (), s32[]{:S(2)}) async-start(), calls=%async_computation.17 | async-start | bytes 10616832 | tf_op jit(solution)/shard_map/all_gather | solution.py:28
  16.8 336.1 %all-gather.19.cloned.1.call-start = ((), (), s32[]{:S(2)}) async-start(), calls=%async_computation.15 | async-start | bytes 10616832 | tf_op jit(solution)/shard_map/all_gather | solution.py:28
  17.4 715.3 %reduce-scatter.15.cloned.1.call-start = ((), (), s32[]{:S(2)}) async-start(), calls=%async_computation.10 | async-start | bytes 10616832 | tf_op jit(solution)/shard_map/reduce_scatter | solution.py:31
  20.6 161.6 %copy-start = (bf16[1,2048,768]{1,2,0:T(8,128)(2,1)}, bf16[1,2048,768]{1,2,0:T(8,128)(2,1)S(1)}, u32[]{:S(2)}) copy-start(bf16[1,2048,768]{1,2,0:T(8,128)(2,1)S(1)} %copy.10) | copy-start | bytes 9437188
  22.2 103.4 %copy-start.10 = (f32[2048]{0:T(1024)}, f32[2048]{0:T(1024)S(1)}, u32[]{:S(2)}) copy-start(f32[2048]{0:T(1024)S(1)} %fusion.78) | copy-start | bytes 24580
  209.4 55.9 %copy-start.14 = (f32[2048]{0:T(1024)}, f32[2048]{0:T(1024)S(1)}, u32[]{:S(2)}) copy-start(f32[2048]{0:T(1024)S(1)} %get-tuple-element.22) | copy-start | bytes 24580
  209.4 267.3 %copy-start.12 = (f32[2048]{0:T(1024)}, f32[2048]{0:T(1024)S(1)}, u32[]{:S(2)}) copy-start(f32[2048]{0:T(1024)S(1)} %fusion.79) | copy-start | bytes 24580
  209.4 86.4 %copy-start.6 = (bf16[2048,768]{0,1:T(8,128)(2,1)S(1)}, bf16[2048,768]{0,1:T(8,128)(2,1)}, u32[]{:S(2)}) copy-start(bf16[2048,768]{0,1:T(8,128)(2,1)} %get-tuple-element.23) | copy-start | bytes 9437188
  449.8 26.8 %copy-start.15 = (f32[2048]{0:T(1024)S(1)}, f32[2048]{0:T(1024)}, u32[]{:S(2)}) copy-start(f32[2048]{0:T(1024)} %copy-done.14) | copy-start | bytes 24580
  449.8 26.9 %copy-start.2 = (bf16[1,2048,768]{1,2,0:T(8,128)(2,1)S(1)}, bf16[1,2048,768]{1,2,0:T(8,128)(2,1)}, u32[]{:S(2)}) copy-start(bf16[1,2048,768]{1,2,0:T(8,128)(2,1)} %copy.9) | copy-start | bytes 9437188
  507.1 225.6 %reduce-scatter.17.cloned.1.call-start = ((), (), s32[]{:S(2)}) async-start(), calls=%async_computation.11 | async-start | bytes 10616832 | tf_op jit(solution)/shard_map/reduce_scatter | solution.py:31
  551.0 181.7 %reduce-scatter.11.cloned.1.call-start = ((), (), s32[]{:S(2)}) async-start(), calls=%async_computation.8 | async-start | bytes 10616832 | tf_op jit(solution)/shard_map/reduce_scatter | solution.py:31
  551.1 63.8 %copy-start.1 = (bf16[1,2048,768]{1,2,0:T(8,128)(2,1)S(1)}, bf16[1,2048,768]{1,2,0:T(8,128)(2,1)}, u32[]{:S(2)}) copy-start(bf16[1,2048,768]{1,2,0:T(8,128)(2,1)} %copy-done) | copy-start | bytes 9437188
  551.1 63.8 %copy-start.11 = (f32[2048]{0:T(1024)S(1)}, f32[2048]{0:T(1024)}, u32[]{:S(2)}) copy-start(f32[2048]{0:T(1024)} %copy-done.10) | copy-start | bytes 24580
  647.0 151.1 %reduce-scatter.13.cloned.1.call-start = ((), (), s32[]{:S(2)}) async-start(), calls=%async_computation.9 | async-start | bytes 10616832 | tf_op jit(solution)/shard_map/reduce_scatter | solution.py:31
  680.8 191.0 %reduce-scatter.9.cloned.1.call-start = ((), (), s32[]{:S(2)}) async-start(), calls=%async_computation.7 | async-start | bytes 10616832 | tf_op jit(solution)/shard_map/reduce_scatter | solution.py:31
  707.1 238.2 %reduce-scatter.7.cloned.1.call-start = ((), (), s32[]{:S(2)}) async-start(), calls=%async_computation.6 | async-start | bytes 10616832 | tf_op jit(solution)/shard_map/reduce_scatter | solution.py:31
  732.6 382.1 %all-reduce.3.cloned.1.call-start = ((), (), s32[]{:S(2)}) async-start(), calls=%async_computation.18 | async-start | bytes 14155776 | tf_op jit(solution)/shard_map/psum | solution.py:31
  978.3 26.9 %copy-start.9 = (f32[2048]{0:T(1024)S(1)}, f32[2048]{0:T(1024)}, u32[]{:S(2)}) copy-start(f32[2048]{0:T(1024)} %copy-done.8) | copy-start | bytes 24580
  978.3 26.9 %copy-start.4 = (bf16[2048,768]{0,1:T(8,128)(2,1)S(1)}, bf16[2048,768]{0,1:T(8,128)(2,1)}, u32[]{:S(2)}) copy-start(bf16[2048,768]{0,1:T(8,128)(2,1)} %copy-done.3) | copy-start | bytes 9437188
  (5 other events, 12.0 us)
Sparse Core Ops, SparseCore 0:
  10.8 57.5 all-gather.12
  70.8 54.7 all-gather.14
  127.5 54.7 all-gather.16
  183.9 54.7 all-gather.20
  241.0 54.7 all-gather.22
  298.1 54.7 all-gather.18
  507.3 70.1 reduce-scatter.14
  580.9 70.1 reduce-scatter.16
  654.5 70.1 reduce-scatter.10
  728.0 70.1 reduce-scatter.12
  801.6 70.1 reduce-scatter.8
  875.1 70.1 reduce-scatter.6
  948.4 166.2 all-reduce.2
where the time goes:
time: 1140 us; the launch traced here: 1130 us
  matrix products  595 us (52%)
  waiting for transfers between devices  479 us (42%)
  local copies, waits for them, and re-layouts  25.8 us (2%)
  between operations  14.5 us (1%)
  other arithmetic  14.1 us (1%)
    reduce_scatter x6, waiting for transfers between devices, summed(): lax.psum_scatter(term, 's', scatter_dimension=0, tiled=True)  213 us
    dot_general x6, matrix products, layer(): up = jnp.dot(a, w['w_up'], preferred_element_type=jnp.float32)  211 us
    dot_general x6, matrix products, layer(): gate = jnp.dot(a, w['w_gate'], preferred_element_type=jnp.float32)  198 us
    dot_general x5, matrix products, matmul(): jnp.dot(a, w, preferred_element_type=jnp.float32).astype(jnp.bfloat16)  186 us
    all_gather x6, waiting for transfers between devices, fetched(): lax.all_gather(w[number], 's', axis=0, tiled=True)  164 us
    psum x1, waiting for transfers between devices, summed(): lax.psum(lax.psum_scatter(term, 's', scatter_dimension=0, tiled=True), 'r')  101 us
  transfers between devices with their start and end apart: 13, of which 10 were waited for; matrix products, arithmetic and copies ran while one was open for 41% of the time, Pallas kernels for 0%

commit v1 on v0

v1 whole, which is shorter than its diff:
```python
import functools

import jax
import jax.numpy as jnp
from jax import lax
from jax.experimental import pallas as pl
from jax.experimental.pallas import tpu as pltpu
from jax.sharding import PartitionSpec as P

MESH = pl.DeviceIdType.MESH
BF, F32 = jnp.bfloat16, jnp.float32
J = 6
TILES = 4


def nn(a, b):
    return lax.dot_general(a, b, (((1,), (0,)), ((), ())), preferred_element_type=F32)


def nt(a, b):
    return lax.dot_general(a, b, (((1,), (1,)), ((), ())), preferred_element_type=F32)


def kernel(
    x_ref, dy_ref, gu_ref, wd_ref,
    dx_ref, out_ref, g_ref, d_ref, h_ref,
    a, at, dy, dyt, acc, guv, wdv, mid, dg, du, term, r1, r2, r3, r4,
    ag_recv, ag_send, load_sem, s1, s2, s3, s4, out_sem, io_sem,
):
    tokens, width = a.shape
    rows = tokens // TILES
    U = 2 * J
    r, s = lax.axis_index("r"), lax.axis_index("s")
    c, y, x = s % 2, (s // 2) % 2, s // 4
    xy = s // 2
    partner, xn, yn = s + 1 - 2 * c, s + 4 - 8 * x, s + 2 - 4 * y
    dev_p, dev_x, dev_y, dev_z = {"s": partner}, {"s": xn}, {"s": yn}, {"r": 1 - r}
    dev_1 = {"s": xn * (1 - r) + yn * r}
    dev_2 = {"s": xn * r + yn * (1 - r)}
    pos1 = xy + (1 - r) * (2 - 4 * x) + r * (1 - 2 * y)
    pos2 = xy + r * (2 - 4 * x) + (1 - r) * (1 - 2 * y)
    pos3 = 3 - xy

    def remote(src, dst, send, recv, dev):
        return pltpu.make_async_remote_copy(src_ref=src, dst_ref=dst, send_sem=send, recv_sem=recv, device_id=dev, device_id_type=MESH)

    def pieces(u, pos, own):
        if own:
            return (gu_ref.at[u], wd_ref.at[u])
        return (g_ref.at[u, pos, c], d_ref.at[u, pos, c])

    def send_block(u, pos, own, kind, dev):
        for i, (src, dst) in enumerate(zip(pieces(u, pos, own), (g_ref.at[u, pos, c], d_ref.at[u, pos, c]))):
            remote(src, dst, ag_send.at[u, 1 if kind == 3 else 0, i], ag_recv.at[u, kind, i], dev).start()

    def wait_block(u, pos, kind):
        for i, ref in enumerate((g_ref.at[u, pos, c], d_ref.at[u, pos, c])):
            remote(ref, ref, ag_send.at[u, 0, i], ag_recv.at[u, kind, i], dev_1).wait_recv()

    def hop(u):
        send_block(u, xy, True, 0, dev_1)

    def forward(u):
        send_block(u, xy, True, 3, dev_p)
        wait_block(u, pos1, 0)
        send_block(u, pos1, False, 1, dev_2)
        send_block(u, pos1, False, 2, dev_z)
        send_block(u, pos1, False, 3, dev_p)

    def across(u):
        wait_block(u, pos2, 2)
        send_block(u, pos2, False, 3, dev_p)
        wait_block(u, pos3, 1)
        send_block(u, pos3, False, 3, dev_p)

    def arrived(u):
        for i, ref in enumerate((g_ref.at[u, :, 1 - c], d_ref.at[u, :, 1 - c])):
            remote(ref, ref, ag_send.at[u, 1, i], ag_recv.at[u, 3, i], dev_p).wait_recv()

    def sent(u):
        for i, ref in enumerate((g_ref, d_ref)):
            three, four = ref.at[u, pl.ds(0, 3), 0], ref.at[u, :, 0]
            remote(three, three, ag_send.at[u, 0, i], ag_recv.at[u, 0, i], dev_1).wait_send()
            remote(four, four, ag_send.at[u, 1, i], ag_recv.at[u, 3, i], dev_p).wait_send()

    def load(u, slot):
        for i, (own, all_, to) in enumerate(((gu_ref, g_ref, guv), (wd_ref, d_ref, wdv))):
            sem = load_sem.at[slot, i]
            pltpu.make_async_copy(own.at[u], to.at[slot, xy, c], sem).start()
            for pos in (pos1, pos2, pos3):
                pltpu.make_async_copy(all_.at[u, pos, c], to.at[slot, pos, c], sem).start()
            pltpu.make_async_copy(all_.at[u, :, 1 - c], to.at[slot, :, 1 - c], sem).start()

    def loaded(slot):
        for i, (all_, to) in enumerate(((g_ref, guv), (d_ref, wdv))):
            pltpu.make_async_copy(all_.at[0], to.at[slot], load_sem.at[slot, i]).wait()

    def gate_half(slot, which, half):
        w = guv[slot, :, :, which, :, pl.ds(512 * half, 512)]
        return w.reshape(width, 512)

    def down_half(slot, half):
        return wdv[slot, pl.ds(2 * half, 2)].reshape(512, width)

    def io(src, dst):
        copy = pltpu.make_async_copy(src, dst, io_sem)
        copy.start()
        copy.wait()

    def tile(m):
        return pl.ds(pl.multiple_of(m * rows, rows), rows)

    def scale_of(h):
        wide = h.astype(F32)
        return wide, lax.rsqrt(jnp.mean(wide * wide, -1, keepdims=True) + 1e-6)

    def put_normed(m, h, plain, turned):
        wide, scale = scale_of(h)
        out = (wide * scale).astype(BF)
        if plain:
            a[tile(m), :] = out
        if turned:
            at[:, tile(m)] = out.T

    def norm_back(m, h):
        wide, scale = scale_of(h)
        by_a = acc[tile(m), :].astype(BF).astype(F32)
        by_scale = jnp.sum(by_a * wide, -1, keepdims=True)
        by_h = by_a * scale - wide * (scale * scale * scale * by_scale * (1.0 / width))
        return (dy[tile(m), :].astype(F32) + by_h.astype(BF).astype(F32)).astype(BF)

    def add(to, term_):
        to[...] = (to[...].astype(F32) + term_[...].astype(F32)).astype(BF)

    H = 384

    def c1(slot):
        return remote(term.at[1 - c], r1.at[slot], s1.at[0, slot], s1.at[1, slot], dev_p)

    def c2(slot):
        return (
            remote(r1.at[slot, 1 - x, :, :, pl.ds(0, H)], r2.at[slot, 0], s2.at[0, slot, 0], s2.at[1, slot, 0], dev_x),
            remote(r1.at[slot, :, 1 - y, :, pl.ds(H, H)], r2.at[slot, 1], s2.at[0, slot, 1], s2.at[1, slot, 1], dev_y),
        )

    def c3(slot):
        return (
            remote(r2.at[slot, 0, 1 - y], r3.at[slot, 0], s3.at[0, slot, 0], s3.at[1, slot, 0], dev_y),
            remote(r2.at[slot, 1, 1 - x], r3.at[slot, 1], s3.at[0, slot, 1], s3.at[1, slot, 1], dev_x),
        )

    def c4(slot):
        return remote(r3.at[slot], r4.at[slot], s4.at[0, slot], s4.at[1, slot], dev_z)

    def written(slot):
        return pltpu.make_async_copy(r4.at[slot], out_ref.at[0], out_sem.at[slot])

    def stage1(t):
        slot = t % 2
        c1(slot).wait()
        for i in range(2):
            for k in range(2):
                add(r1.at[slot, i, k], term.at[c, i, k])
        for copy in c2(slot):
            copy.start()

    def stage2(t):
        slot = t % 2
        for copy in c2(slot):
            copy.wait()
        for k in range(2):
            add(r2.at[slot, 0, k], r1.at[slot, x, k, :, pl.ds(0, H)])
            add(r2.at[slot, 1, k], r1.at[slot, k, y, :, pl.ds(H, H)])
        for copy in c3(slot):
            copy.start()

    def stage3(t):
        slot = t % 2
        for copy in c3(slot):
            copy.wait()
        add(r3.at[slot, 0], r2.at[slot, 0, y])
        add(r3.at[slot, 1], r2.at[slot, 1, x])
        c4(slot).start()

    def stage4(t):
        slot = t % 2
        c4(slot).wait()
        add(r4.at[slot], r3.at[slot])
        u = (t + J) % U
        pltpu.make_async_copy(r4.at[slot], out_ref.at[u], out_sem.at[slot]).start()

    def early(t):
        @pl.when((t >= 3) & (t < U + 3))
        def _():
            written((t - 3) % 2).wait()

        @pl.when((t >= 2) & (t < U + 2))
        def _():
            stage3(t - 2)

        @pl.when((t >= 1) & (t < U + 1))
        def _():
            stage1(t - 1)

    def late(t):
        @pl.when((t >= 2) & (t < U + 2))
        def _():
            stage4(t - 2)

        @pl.when((t >= 1) & (t < U + 1))
        def _():
            stage2(t - 1)

        @pl.when(t < U)
        def _():
            c1(t % 2).start()

    barrier = pltpu.get_barrier_semaphore()
    for dev in (dev_p, dev_x, dev_y, dev_z):
        pl.semaphore_signal(barrier, inc=1, device_id=dev, device_id_type=MESH)
    pl.semaphore_wait(barrier, 4)

    @pl.loop(0, U)
    def _(u):
        hop(u)

    io(x_ref, dy)

    @pl.loop(0, TILES)
    def _(m):
        put_normed(m, dy[tile(m), :], True, False)
        acc[tile(m), :] = jnp.zeros((rows, width), F32)

    forward(0)
    forward(1)
    across(0)
    arrived(0)
    load(0, 0)

    @pl.loop(0, J)
    def _(u):
        slot = u % 2
        loaded(slot)

        def part(half, start, stop):
            @pl.loop(start, stop)
            def _(m):
                gate = nn(a[tile(m), :], gate_half(slot, 0, half))
                up = nn(a[tile(m), :], gate_half(slot, 1, half))
                hidden = (gate * jax.nn.sigmoid(gate) * up).astype(BF)
                acc[tile(m), :] += nn(hidden, down_half(slot, half))

        part(0, 0, TILES)
        forward(u + 2)
        across(u + 1)
        part(1, 0, TILES)
        arrived(u + 1)
        load(u + 1, 1 - slot)

    @pl.loop(0, TILES)
    def _(m):
        h = (dy[tile(m), :].astype(F32) + acc[tile(m), :].astype(BF).astype(F32)).astype(BF)
        dy[tile(m), :] = h
        put_normed(m, h, True, True)
        acc[tile(m), :] = jnp.zeros((rows, width), F32)

    io(dy, h_ref)
    io(dy_ref, dy)

    @pl.loop(0, TILES)
    def _(m):
        dyt[:, tile(m)] = dy[tile(m), :].T

    @pl.loop(0, U)
    def _(t):
        slot = t % 2

        @pl.when(t == J)
        def _():
            io(h_ref, a)

            @pl.loop(0, TILES)
            def _(m):
                out = norm_back(m, a[tile(m), :])
                dy[tile(m), :] = out
                dyt[:, tile(m)] = out.T
                acc[tile(m), :] = jnp.zeros((rows, width), F32)

            io(x_ref, a)

            @pl.loop(0, TILES)
            def _(m):
                put_normed(m, a[tile(m), :], True, True)

        loaded(slot)

        def hidden(half):
            @pl.loop(0, TILES)
            def _(m):
                gate = nn(a[tile(m), :], gate_half(slot, 0, half))
                up = nn(a[tile(m), :], gate_half(slot, 1, half))
                by_mid = nt(dy[tile(m), :], down_half(slot, half)).astype(BF).astype(F32)
                sig = jax.nn.sigmoid(gate)
                silu = gate * sig
                mid[tile(m), :] = (silu * up).astype(BF)
                du[tile(m), :] = (by_mid * silu).astype(BF)
                dg[tile(m), :] = (by_mid * up * (sig + silu * (1.0 - sig))).astype(BF)

        def weights(half):
            @pl.loop(0, 2)
            def _(n):
                cols = pl.ds(pl.multiple_of(n * 256, 256), 256)
                for which, of in enumerate((dg, du)):
                    out = nn(at[...], of[:, cols]).astype(BF)
                    for k in range(2):
                        place = pl.ds(pl.multiple_of(96 * (4 * half + k) + 192 * n, 32), 96)
                        for to in range(8):
                            term[to % 2, to // 4, (to // 2) % 2, which, place, :] = out[96 * to : 96 * to + 96, 128 * k : 128 * k + 128]
                out = nn(dyt[...], mid[:, cols]).astype(BF)
                for k in range(2):
                    term[k, half, n, 2] = out[:, 128 * k : 128 * k + 128]

        def states(half):
            @pl.loop(0, TILES)
            def _(m):
                acc[tile(m), :] += nt(dg[tile(m), :], gate_half(slot, 0, half)) + nt(du[tile(m), :], gate_half(slot, 1, half))

        hidden(0)
        early(t)

        @pl.when(t < 2)
        def _():
            forward(J + 2 + 2 * t)

        @pl.when(t < 3)
        def _():
            across(J + 1 + 2 * t)

        weights(0)
        states(0)

        @pl.when(t < J - 1)
        def _():
            arrived(J + 1 + t)

        @pl.when(t < U - 1)
        def _():
            load((J + 1 + t) % U, 1 - slot)

        @pl.when(t < 2)
        def _():
            forward(J + 3 + 2 * t)
            across(J + 2 + 2 * t)

        hidden(1)
        weights(1)
        late(t)
        states(1)

    early(U)
    io(x_ref, a)

    @pl.loop(0, TILES)
    def _(m):
        dy[tile(m), :] = norm_back(m, a[tile(m), :])

    io(dy, dx_ref)
    late(U)
    early(U + 1)
    late(U + 1)
    early(U + 2)
    for u in range(U):
        sent(u)


def solution(mesh):
    def step(x, dy, w_gate, w_up, w_down):
        tokens, width = x.shape[1:]
        layers, own, ff = w_gate.shape
        U = layers * J

        def chunked(w):
            return w.reshape(layers, own, 8, J, 128).transpose(0, 3, 1, 2, 4).reshape(U, own, 1024)

        gu = jnp.stack([chunked(w_gate), chunked(w_up)], 1)
        wd = w_down.reshape(U, 128, width)
        hbm = pl.BlockSpec(memory_space=pl.ANY)
        vmem, dma = pltpu.VMEM, pltpu.SemaphoreType.DMA
        dx, out, *_ = pl.pallas_call(
            kernel,
            in_specs=[hbm] * 4,
            out_specs=[hbm] * 5,
            out_shape=[
                jax.ShapeDtypeStruct((tokens, width), BF),
                jax.ShapeDtypeStruct((U, 2, 3, 384, 128), BF),
                jax.ShapeDtypeStruct((U, 4, 2, 2, own, 1024), BF),
                jax.ShapeDtypeStruct((U, 4, 2, 128, width), BF),
                jax.ShapeDtypeStruct((tokens, width), BF),
            ],
            scratch_shapes=[
                vmem((tokens, width), BF),
                vmem((width, tokens), BF),
                vmem((tokens, width), BF),
                vmem((width, tokens), BF),
                vmem((tokens, width), F32),
                vmem((2, 4, 2, 2, own, 1024), BF),
                vmem((2, 4, 2, 128, width), BF),
                vmem((tokens, 512), BF),
                vmem((tokens, 512), BF),
                vmem((tokens, 512), BF),
                vmem((2, 2, 2, 3, 768, 128), BF),
                vmem((2, 2, 2, 3, 768, 128), BF),
                vmem((2, 2, 2, 3, 384, 128), BF),
                vmem((2, 2, 3, 384, 128), BF),
                vmem((2, 2, 3, 384, 128), BF),
                dma((U, 4, 2)),
                dma((U, 2, 2)),
                dma((2, 2)),
                dma((2, 2)),
                dma((2, 2, 2)),
                dma((2, 2, 2)),
                dma((2, 2)),
                dma((2,)),
                dma,
            ],
            compiler_params=pltpu.CompilerParams(collective_id=0, has_side_effects=True, vmem_limit_bytes=67043328),
            name="stack",
        )(x[0], dy[0], gu, wd)
        out = out.reshape(layers, J, 2, 3, 4, own, 128)

        def rows_of(which):
            return out[:, :, :, which].transpose(0, 4, 2, 3, 1, 5).reshape(layers, own, ff)

        down = out[:, :, :, 2].reshape(layers, J, width, 128).transpose(0, 1, 3, 2).reshape(layers, J * 128, width)
        return dx[None], rows_of(0), rows_of(1), down

    states, cut = P(("rep", "r", "s"), None, None), P(None, "s", None)
    return jax.shard_map(
        step,
        mesh=mesh,
        in_specs=(states, states) + (cut,) * 3,
        out_specs=(states,) + (P("rep", "s", None),) * 3,
        check_vma=False,
    )
```

time: 1140 us -> 655 us (0.57)
  Pallas kernels: 0 us -> 596 us
  matrix products: 595 us -> 0 us
  waiting for transfers between devices: 479 us -> 0 us
  local copies, waits for them, and re-layouts: 25.8 us -> 53.6 us
  between operations: 14.5 us -> 0.66 us
    pallas_call x0 -> x1, Pallas kernels: none -> 596 us  [step(): pl.pallas_call(kernel, in_specs=[hbm] * 4, out_specs=[hbm] * 5, out_shape...]
    dot_general x17 -> x0, matrix products: 595 us -> none  [the longest x6 211 us: layer(): up = jnp.dot(a, w['w_up'], preferred_element_type=jnp.float32)]
    reduce_scatter x6 -> x0, waiting for transfers between devices: 213 us -> none  [summed(): lax.psum_scatter(term, 's', scatter_dimension=0, tiled=True)]
    all_gather x6 -> x0, waiting for transfers between devices: 164 us -> none  [fetched(): lax.all_gather(w[number], 's', axis=0, tiled=True)]
    psum x1 -> x0, waiting for transfers between devices: 101 us -> none  [summed(): lax.psum(lax.psum_scatter(term, 's', scatter_dimension=0, tiled=True), 'r')]
    reshape x0 -> x4, local copies, waits for them, and re-layouts: none -> 19.3 us  [the longest x2 9.88 us: chunked(): w.reshape(layers, own, 8, J, 128).transpose(0, 3, 1, 2, 4)]
    unnamed x35 -> x3, local copies, waits for them, and re-layouts: 17.6 us -> 3.76 us
    another operation x0 -> x3, local copies, waits for them, and re-layouts: none -> 12.5 us  [the longest x2 10 us: step(): gu = jnp.stack([chunked(w_gate), chunked(w_up)], 1)]
  transfers between devices with their start and end apart: 13 -> 0, of which waited for: 10 -> 0; matrix products, arithmetic and copies ran while one was open for 41% -> 0% of each run, Pallas kernels for 0% -> 0%
where the time goes in v1:
time: 655 us; the launch traced here: 654 us
  Pallas kernels  596 us (91%)
  local copies, waits for them, and re-layouts  53.6 us (8%)
    pallas_call x1, Pallas kernels, step(): pl.pallas_call(kernel, in_specs=[hbm] * 4, out_specs=[hbm] * 5, out_shape...  596 us

profile of v1, /device:TPU:0, one launch (start us, length us, event | category | flops | bytes accessed | tf_op | source)
XLA Modules:
  0.0 654.2 jit_solution(14860524671035986971)
XLA Ops:
  0.6 4.9 reshape.29
  5.6 1.8 copy.14
  7.3 4.9 stack_reshape.6
  12.3 4.9 reshape.30
  17.2 1.8 copy.15
  19.0 0.0 copy-start
  19.0 5.1 stack_reshape.7
  24.1 0.0 copy-done
  24.1 4.2 pad_maximum_fusion.gu_ref
  28.3 595.7 %stack.5 = (bf16[2048,768]{1,0:T(8,128)(2,1)}, bf16[12,2,3,384,128]{4,3,2,1,0:T(8,128)(2,1)}, bf16[12,4,2,2,96,1024]{5,4,3,2,1,0:T(8,128)(2,1)}, bf16[12,4,2,128,768]{4,3,2,1,0:T(8,128)(2,1)}, bf16[2048,768]{1,0:T(8,128)(2,1)}) custom-call(bf16[2048,768]{1,0:T(8,128)(2,1)} %bitcast.28, bf16[2048,768]{1,0:T(8,128)(2,1)} %bitcast.29, ...), custom_call_target="tpu_custom_call" | custom-call | tf_op jit(solution)/shard_map/stack/pallas_call | solution.py:389
  624.0 7.2 %fusion = (bf16[2,6,2,1,4,96,128]{6,5,4,3,2,1,0:T(8,128)(2,1)S(1)}, bf16[2,6,2,1,4,96,128]{6,5,4,3,2,1,0:T(8,128)(2,1)}, bf16[2,6,2,1,4,96,128]{6,5,4,3,2,1,0:T(8,128)(2,1)}) fusion(bf16[2,6,2,3,4,96,128]{6,5,4,3,2,1,0:T(8,128)(2,1)} %bitcast.26), kind=kLoop, calls=%fused_computation.3 | loop fusion | bytes 14155776 | tf_op jit(solution)/shard_map/slice | solution.py:434
  631.3 2.4 copy.18
  633.7 7.3 %copy_bitcast_fusion = (bf16[2,96,2,4,6,128]{5,4,3,2,1,0:T(8,128)(2,1)}, bf16[2,96,2,4,6,128]{5,4,3,2,1,0:T(8,128)(2,1)S(1)}) fusion(bf16[2,6,2,1,4,96,128]{6,5,4,3,2,1,0:T(8,128)(2,1)} %get-tuple-element.10, bf16[2,6,2,1,4,96,128]{6,5,4,3,2,1,0:T(8,128)(2,1)} %get-tuple-element.9), kind=kLoop, calls=%fused_computation.1 | loop fusion | bytes 9437184 | tf_op jit(solution)/shard_map/transpose | solution.py:432
  641.0 5.9 reshape.34
  646.9 3.6 reshape.33
  650.4 3.8 copy.24
Async XLA Ops:
  19.0 5.1 copy-start

commit v2 on v1

--- a/solution.py
+++ b/solution.py
@@ -22,10 +22,10 @@
 
 
 def kernel(
-    x_ref, dy_ref, gu_ref, wd_ref,
-    dx_ref, out_ref, g_ref, d_ref, h_ref,
-    a, at, dy, dyt, acc, guv, wdv, mid, dg, du, term, r1, r2, r3, r4,
-    ag_recv, ag_send, load_sem, s1, s2, s3, s4, out_sem, io_sem,
+    x_ref, dy_ref, wg_ref, wu_ref, wd_ref,
+    dx_ref, dwg_ref, dwu_ref, dwd_ref, g_ref, d_ref, h_ref, save_ref, mid_ref,
+    a, at, dy, dyt, acc, guv, wdv, mid, dgu, term, r1, r2, r3, r4, shard, turned, pair,
+    ag_recv, ag_send, load_sem, s1, s2, s3, s4, out_sem, io_sem, shard_sem, save_sem, mid_sem,
 ):
     tokens, width = a.shape
     rows = tokens // TILES
@@ -44,10 +44,11 @@
     def remote(src, dst, send, recv, dev):
         return pltpu.make_async_remote_copy(src_ref=src, dst_ref=dst, send_sem=send, recv_sem=recv, device_id=dev, device_id_type=MESH)
 
+    def down_own(u):
+        return wd_ref.at[u // J, pl.ds(pl.multiple_of(128 * (u % J), 128), 128)]
+
     def pieces(u, pos, own):
-        if own:
-            return (gu_ref.at[u], wd_ref.at[u])
-        return (g_ref.at[u, pos, c], d_ref.at[u, pos, c])
+        return (g_ref.at[u, pos, c], down_own(u) if own else d_ref.at[u, pos, c])
 
     def send_block(u, pos, own, kind, dev):
         for i, (src, dst) in enumerate(zip(pieces(u, pos, own), (g_ref.at[u, pos, c], d_ref.at[u, pos, c]))):
@@ -84,12 +85,12 @@
             remote(four, four, ag_send.at[u, 1, i], ag_recv.at[u, 3, i], dev_p).wait_send()
 
     def load(u, slot):
-        for i, (own, all_, to) in enumerate(((gu_ref, g_ref, guv), (wd_ref, d_ref, wdv))):
-            sem = load_sem.at[slot, i]
-            pltpu.make_async_copy(own.at[u], to.at[slot, xy, c], sem).start()
-            for pos in (pos1, pos2, pos3):
-                pltpu.make_async_copy(all_.at[u, pos, c], to.at[slot, pos, c], sem).start()
-            pltpu.make_async_copy(all_.at[u, :, 1 - c], to.at[slot, :, 1 - c], sem).start()
+        pltpu.make_async_copy(g_ref.at[u], guv.at[slot], load_sem.at[slot, 0]).start()
+        sem = load_sem.at[slot, 1]
+        pltpu.make_async_copy(down_own(u), wdv.at[slot, xy, c], sem).start()
+        for pos in (pos1, pos2, pos3):
+            pltpu.make_async_copy(d_ref.at[u, pos, c], wdv.at[slot, pos, c], sem).start()
+        pltpu.make_async_copy(d_ref.at[u, :, 1 - c], wdv.at[slot, :, 1 - c], sem).start()
 
     def loaded(slot):
         for i, (all_, to) in enumerate(((g_ref, guv), (d_ref, wdv))):
@@ -152,8 +153,14 @@
     def c4(slot):
         return remote(r3.at[slot], r4.at[slot], s4.at[0, slot], s4.at[1, slot], dev_z)
 
-    def written(slot):
-        return pltpu.make_async_copy(r4.at[slot], out_ref.at[0], out_sem.at[slot])
+    def written(slot, u=0):
+        return pltpu.make_async_copy(turned.at[slot], down_grad(u), out_sem.at[slot])
+
+    def down_grad(u):
+        return dwd_ref.at[u // J, pl.ds(pl.multiple_of(128 * (u % J), 128), 128)]
+
+    def layer_written(layer):
+        return [pltpu.make_async_copy(shard.at[layer, i], to.at[layer], shard_sem.at[layer, i]) for i, to in enumerate((dwg_ref, dwu_ref))]
 
     def stage1(t):
         slot = t % 2
@@ -185,9 +192,22 @@
     def stage4(t):
         slot = t % 2
         c4(slot).wait()
-        add(r4.at[slot], r3.at[slot])
         u = (t + J) % U
-        pltpu.make_async_copy(r4.at[slot], out_ref.at[u], out_sem.at[slot]).start()
+        for half in range(2):
+            for i in range(2):
+                for k in range(4):
+                    own = pl.ds(96 * k, 96)
+                    total = r4[slot, half, i, own].astype(F32) + r3[slot, half, i, own].astype(F32)
+                    lanes = pl.ds(pl.multiple_of(768 * (4 * half + k) + 128 * (u % J), 128), 128)
+                    shard[u // J, i, :, lanes] = total.astype(BF)
+            total = r4[slot, half, 2].astype(F32) + r3[slot, half, 2].astype(F32)
+            turned[slot, :, H * half : H * half + H] = total.astype(BF).T
+        written(slot, u).start()
+
+        @pl.when(u % J == J - 1)
+        def _():
+            for copy in layer_written(u // J):
+                copy.start()
 
     def early(t):
         @pl.when((t >= 3) & (t < U + 3))
@@ -220,11 +240,37 @@
         pl.semaphore_signal(barrier, inc=1, device_id=dev, device_id_type=MESH)
     pl.semaphore_wait(barrier, 4)
 
-    @pl.loop(0, U)
-    def _(u):
-        hop(u)
-
-    io(x_ref, dy)
+    def fetched(layer):
+        return [pltpu.make_async_copy(ref.at[layer], shard.at[layer, i], shard_sem.at[layer, i]) for i, ref in enumerate((wg_ref, wu_ref))]
+
+    fetching = [copy for layer in range(2) for copy in fetched(layer)]
+    for copy in fetching:
+        copy.start()
+    getting = pltpu.make_async_copy(x_ref, dy, io_sem)
+    getting.start()
+
+    for layer in range(2):
+        for i in range(2):
+            fetching[2 * layer + i].wait()
+
+        @pl.loop(0, J)
+        def _(j):
+            u = J * layer + j
+            block = guv.at[u // 8, (u // 2) % 4, u % 2]
+            for i in range(2):
+                for k in range(8):
+                    lanes = pl.ds(pl.multiple_of(768 * k + 128 * j, 128), 128)
+                    block[i, :, 128 * k : 128 * k + 128] = shard[layer, i, :, lanes]
+
+        puts = []
+        for u in range(J * layer, J * layer + J):
+            puts.append(pltpu.make_async_copy(guv.at[u // 8, (u // 2) % 4, u % 2], g_ref.at[u, xy, c], save_sem.at[u]))
+            puts[-1].start()
+        for u in range(J * layer, J * layer + J):
+            puts[u - J * layer].wait()
+            hop(u)
+
+    getting.wait()
 
     @pl.loop(0, TILES)
     def _(m):
@@ -237,6 +283,15 @@
     arrived(0)
     load(0, 0)
 
+    def saved(u, half, m):
+        return (
+            pltpu.make_async_copy(pair.at[m % 2], save_ref.at[u, half, m], save_sem.at[m % 2]),
+            pltpu.make_async_copy(mid.at[tile(m)], mid_ref.at[u, half, tile(m)], mid_sem.at[m % 2]),
+        )
+
+    def restored(u, half, m):
+        return pltpu.make_async_copy(save_ref.at[u, half, m], pair.at[m % 2], save_sem.at[m % 2])
+
     @pl.loop(0, J)
     def _(u):
         slot = u % 2
@@ -247,8 +302,21 @@
             def _(m):
                 gate = nn(a[tile(m), :], gate_half(slot, 0, half))
                 up = nn(a[tile(m), :], gate_half(slot, 1, half))
-                hidden = (gate * jax.nn.sigmoid(gate) * up).astype(BF)
+
+                @pl.when((u > 0) | (m >= 2) | (half > 0))
+                def _():
+                    for copy in saved(u, half, m):
+                        copy.wait()
+
+                sig = jax.nn.sigmoid(gate)
+                silu = gate * sig
+                hidden = (silu * up).astype(BF)
+                mid[tile(m), :] = hidden
+                pair[m % 2, 0] = silu
+                pair[m % 2, 1] = up * (sig + silu * (1.0 - sig))
                 acc[tile(m), :] += nn(hidden, down_half(slot, half))
+                for copy in saved(u, half, m):
+                    copy.start()
 
         part(0, 0, TILES)
         forward(u + 2)
@@ -257,6 +325,10 @@
         arrived(u + 1)
         load(u + 1, 1 - slot)
 
+    for m in range(2):
+        for copy in saved(0, 0, m):
+            copy.wait()
+
     @pl.loop(0, TILES)
     def _(m):
         h = (dy[tile(m), :].astype(F32) + acc[tile(m), :].astype(BF).astype(F32)).astype(BF)
@@ -290,7 +362,10 @@
 
             @pl.loop(0, TILES)
             def _(m):
-                put_normed(m, a[tile(m), :], True, True)
+                put_normed(m, a[tile(m), :], False, True)
+
+            for m in range(2):
+                restored(0, 0, m).start()
 
         loaded(slot)
 
@@ -303,15 +378,46 @@
                 sig = jax.nn.sigmoid(gate)
                 silu = gate * sig
                 mid[tile(m), :] = (silu * up).astype(BF)
-                du[tile(m), :] = (by_mid * silu).astype(BF)
-                dg[tile(m), :] = (by_mid * up * (sig + silu * (1.0 - sig))).astype(BF)
+                dgu[tile(m), 0:512] = (by_mid * (up * (sig + silu * (1.0 - sig)))).astype(BF)
+                dgu[tile(m), 512:1024] = (by_mid * silu).astype(BF)
+
+        def restore(half):
+            u = t - J
+            getting = pltpu.make_async_copy(mid_ref.at[u, half], mid, mid_sem.at[0])
+            getting.start()
+
+            @pl.loop(0, TILES)
+            def _(m):
+                by_mid = nt(dy[tile(m), :], down_half(slot, half)).astype(BF).astype(F32)
+                restored(u, half, m).wait()
+                dgu[tile(m), 0:512] = (by_mid * pair[m % 2, 1]).astype(BF)
+                dgu[tile(m), 512:1024] = (by_mid * pair[m % 2, 0]).astype(BF)
+
+                @pl.when(m < 2)
+                def _():
+                    restored(u, half, m + 2).start()
+
+                @pl.when((m >= 2) & ((u < J - 1) | (half == 0)))
+                def _():
+                    restored(u + half, 1 - half, m - 2).start()
+
+            getting.wait()
+
+        def products(half):
+            @pl.when(t < J)
+            def _():
+                hidden(half)
+
+            @pl.when(t >= J)
+            def _():
+                restore(half)
 
         def weights(half):
             @pl.loop(0, 2)
             def _(n):
                 cols = pl.ds(pl.multiple_of(n * 256, 256), 256)
-                for which, of in enumerate((dg, du)):
-                    out = nn(at[...], of[:, cols]).astype(BF)
+                for which in range(2):
+                    out = nn(at[...], dgu[:, pl.ds(pl.multiple_of(512 * which + n * 256, 256), 256)]).astype(BF)
                     for k in range(2):
                         place = pl.ds(pl.multiple_of(96 * (4 * half + k) + 192 * n, 32), 96)
                         for to in range(8):
@@ -323,9 +429,10 @@
         def states(half):
             @pl.loop(0, TILES)
             def _(m):
-                acc[tile(m), :] += nt(dg[tile(m), :], gate_half(slot, 0, half)) + nt(du[tile(m), :], gate_half(slot, 1, half))
-
-        hidden(0)
+                both = jnp.concatenate([gate_half(slot, 0, half), gate_half(slot, 1, half)], 1)
+                acc[tile(m), :] += nt(dgu[tile(m), :], both)
+
+        products(0)
         early(t)
 
         @pl.when(t < 2)
@@ -352,13 +459,12 @@
             forward(J + 3 + 2 * t)
             across(J + 2 + 2 * t)
 
-        hidden(1)
+        products(1)
         weights(1)
         late(t)
         states(1)
 
     early(U)
-    io(x_ref, a)
 
     @pl.loop(0, TILES)
     def _(m):
@@ -369,7 +475,12 @@
     early(U + 1)
     late(U + 1)
     early(U + 2)
-    for u in range(U):
+    for layer in range(2):
+        for copy in layer_written(layer):
+            copy.wait()
+
+    @pl.loop(0, U)
+    def _(u):
         sent(u)
 
 
@@ -379,23 +490,20 @@
         layers, own, ff = w_gate.shape
         U = layers * J
 
-        def chunked(w):
-            return w.reshape(layers, own, 8, J, 128).transpose(0, 3, 1, 2, 4).reshape(U, own, 1024)
-
-        gu = jnp.stack([chunked(w_gate), chunked(w_up)], 1)
-        wd = w_down.reshape(U, 128, width)
         hbm = pl.BlockSpec(memory_space=pl.ANY)
         vmem, dma = pltpu.VMEM, pltpu.SemaphoreType.DMA
-        dx, out, *_ = pl.pallas_call(
+        dx, by_gate, by_up, by_down, *_ = pl.pallas_call(
             kernel,
-            in_specs=[hbm] * 4,
-            out_specs=[hbm] * 5,
+            in_specs=[hbm] * 5,
+            out_specs=[hbm] * 9,
             out_shape=[
                 jax.ShapeDtypeStruct((tokens, width), BF),
-                jax.ShapeDtypeStruct((U, 2, 3, 384, 128), BF),
+                *(jax.ShapeDtypeStruct(w.shape, BF) for w in (w_gate, w_up, w_down)),
                 jax.ShapeDtypeStruct((U, 4, 2, 2, own, 1024), BF),
                 jax.ShapeDtypeStruct((U, 4, 2, 128, width), BF),
                 jax.ShapeDtypeStruct((tokens, width), BF),
+                jax.ShapeDtypeStruct((J, 2, TILES, 2, tokens // TILES, 512), F32),
+                jax.ShapeDtypeStruct((J, 2, tokens, 512), BF),
             ],
             scratch_shapes=[
                 vmem((tokens, width), BF),
@@ -406,13 +514,15 @@
                 vmem((2, 4, 2, 2, own, 1024), BF),
                 vmem((2, 4, 2, 128, width), BF),
                 vmem((tokens, 512), BF),
-                vmem((tokens, 512), BF),
-                vmem((tokens, 512), BF),
+                vmem((tokens, 1024), BF),
                 vmem((2, 2, 2, 3, 768, 128), BF),
                 vmem((2, 2, 2, 3, 768, 128), BF),
                 vmem((2, 2, 2, 3, 384, 128), BF),
                 vmem((2, 2, 3, 384, 128), BF),
                 vmem((2, 2, 3, 384, 128), BF),
+                vmem((layers, 2, own, ff), BF),
+                vmem((2, 128, width), BF),
+                vmem((2, 2, tokens // TILES, 512), F32),
                 dma((U, 4, 2)),
                 dma((U, 2, 2)),
                 dma((2, 2)),
@@ -422,17 +532,14 @@
                 dma((2, 2)),
                 dma((2,)),
                 dma,
+                dma((2, 2)),
+                dma((U,)),
+                dma((2,)),
             ],
             compiler_params=pltpu.CompilerParams(collective_id=0, has_side_effects=True, vmem_limit_bytes=67043328),
             name="stack",
-        )(x[0], dy[0], gu, wd)
-        out = out.reshape(layers, J, 2, 3, 4, own, 128)
-
-        def rows_of(which):
-            return out[:, :, :, which].transpose(0, 4, 2, 3, 1, 5).reshape(layers, own, ff)
-
-        down = out[:, :, :, 2].reshape(layers, J, width, 128).transpose(0, 1, 3, 2).reshape(layers, J * 128, width)
-        return dx[None], rows_of(0), rows_of(1), down
+        )(x[0], dy[0], w_gate, w_up, w_down)
+        return dx[None], by_gate, by_up, by_down
 
     states, cut = P(("rep", "r", "s"), None, None), P(None, "s", None)
     return jax.shard_map(

time: 655 us -> 604 us (0.922)
  local copies, waits for them, and re-layouts: 53.6 us -> 10.3 us
    reshape x4 -> x0, local copies, waits for them, and re-layouts: 19.3 us -> none  [the longest x2 9.88 us: chunked(): w.reshape(layers, own, 8, J, 128).transpose(0, 3, 1, 2, 4)]
    another operation x3 -> x0, local copies, waits for them, and re-layouts: 12.5 us -> none  [the longest x2 10 us: step(): gu = jnp.stack([chunked(w_gate), chunked(w_up)], 1)]
    transpose x3 -> x0, local copies, waits for them, and re-layouts: 10.8 us -> none  [the longest x1 7.31 us: rows_of(): out[:, :, :, which].transpose(0, 4, 2, 3, 1, 5).reshape(layers, own, ff)]
    slice x1 -> x0, local copies, waits for them, and re-layouts: 7.24 us -> none  [step(): out[:, :, :, 2].reshape(layers, J, width, 128).transpose(0, 1, 3, 2)]
    unnamed x3 -> x10, local copies, waits for them, and re-layouts: 3.76 us -> 10.3 us
where the time goes in v2:
time: 604 us
  Pallas kernels  593 us (98%)
  local copies, waits for them, and re-layouts  10.3 us (2%)
    pallas_call x1, Pallas kernels, step(): pl.pallas_call(kernel, in_specs=[hbm] * 5, out_specs=[hbm] * 9, out_shape...  593 us

profile of v2, /device:TPU:0, one launch (start us, length us, event | category | flops | bytes accessed | tf_op | source)
XLA Modules:
  0.0 603.7 jit_solution(17439872923223738103)
XLA Ops:
  0.6 592.7 %stack.1 = (bf16[2048,768]{1,0:T(8,128)(2,1)}, bf16[2,96,6144]{2,1,0:T(8,128)(2,1)}, bf16[2,96,6144]{2,1,0:T(8,128)(2,1)}, bf16[2,768,768]{2,1,0:T(8,128)(2,1)},...) custom-call(bf16[2048,768]{1,0:T(8,128)(2,1)} %bitcast.4, ...), custom_call_target="tpu_custom_call" | custom-call | tf_op jit(solution)/shard_map/stack/pallas_call | solution.py:495
  593.3 0.0 copy-start.2
  593.3 3.9 copy.13
  597.3 0.0 copy-done.2
  597.3 0.0 copy-start.1
  597.3 1.4 copy.14
  598.7 1.1 copy-done.1
  599.8 0.0 copy-start
  599.8 1.4 copy.15
  601.2 1.1 copy-done
  602.3 1.4 copy.16
Async XLA Ops:
  593.3 3.9 copy-start.2
  597.3 2.5 copy-start.1
  599.8 2.5 copy-start
